TPU v7x, 512 devices: a whole 4x8x8 slice. The times are simulated.
512 devices in a mesh: inter: 64 (over y, z_hi, core), intra: 8 (over x, z_lo).
Axes of the slice: x: 4, y: 8, z: 8 (z_hi: 4, z_lo: 2; z = z_hi * 2 + z_lo), core: 2. Of those that a mesh axis runs over, the one named last changes fastest.
Arguments:
- hidden_in: bfloat16 [64, 1024, 4096], P('inter', 'intra'), may hold values from -120 to 120, as said below
- norm_gain: bfloat16 [4096], P(('inter', 'intra')), may hold values from 0.5 to 2, as said below
- qkv_weight: bfloat16 [4096, 768], P(('inter', 'intra')), may hold values from -0.09375 to 0.09375
- attn_cotangent: bfloat16 [64, 1024, 512], P('inter', 'intra'), may hold values from -6 to 6
Outputs:
- attn: bfloat16 [64, 1024, 512], P('inter', 'intra')
- grad_in: bfloat16 [64, 1024, 4096], P('inter', 'intra')
- weight_grad: float32 [4096, 768], P(('intra', 'inter'))
- gain_grad: float32 [4096], P(('intra', 'inter'))
Inputs may be any that keep to these rules, and one draw needn't show every extreme that they name: `hidden_in`: activations with spread row and feature scales. `norm_gain`: positive gains.
All inputs are finite; a program needn't handle non-finite values.
Results may differ from a plain program's by a relative error of at most 0.015.
Values may be sent and summed in bfloat16 or wider, within the bound.
A program may use at most 64 MiB of HBM per device.

v0:
```python
import math
import jax
import jax.numpy as jnp
from jax import lax
from jax.sharding import PartitionSpec as P

HD = 128
HEADS = 4
eps_norm = 1e-05
rope_base = 500000.0


def sent_together(arrays, axis, dim, along):
    widths = [math.prod(a.shape[along:]) for a in arrays]
    both = jnp.concatenate(
        [a.reshape(*a.shape[:along], w) for a, w in zip(arrays, widths)], axis=along
    )
    filled = lax.all_gather(both, axis, axis=dim, tiled=True)
    tiles = jnp.split(filled, [sum(widths[:k]) for k in range(1, len(widths))], axis=along)
    return tuple(
        (b.reshape(*filled.shape[:along], *a.shape[along:]) for a, b in zip(arrays, tiles))
    )


def in_one_piece(arrays, axis, dim, along):
    ends, at = ([], 0)
    for a in arrays[:-1]:
        at += a.shape[along]
        ends.append(at)
    both = jnp.concatenate(arrays, axis=along)
    return tuple(jnp.split(lax.all_gather(both, axis, axis=dim, tiled=True), ends, axis=along))


def gather_turned(arrays, axis, dims):
    turned = [jnp.moveaxis(a, dim, 0) for a, dim in zip(arrays, dims)]
    both = jnp.concatenate([t.reshape(len(t), -1) for t in turned], axis=1)
    filled, at, outs = (lax.all_gather(both, axis, axis=0, tiled=True), 0, [])
    for t, dim in zip(turned, dims):
        section = filled[:, at : at + t[0].size].reshape(-1, *t.shape[1:])
        outs.append(jnp.moveaxis(section, 0, dim))
        at += t[0].size
    return tuple(outs)


def in_order(tiles, dim):
    tiles = jnp.moveaxis(tiles, 0, dim)
    dims = tiles.shape
    return tiles.reshape(*dims[:dim], dims[dim] * dims[dim + 1], *dims[dim + 2 :])


def from_everyone(x, axis):
    copies = jnp.broadcast_to(x, (lax.axis_size(axis), *x.shape))
    return lax.all_to_all(copies, axis, split_axis=0, concat_axis=0, tiled=True)


def gather_directly(x, axis, dim):
    return in_order(from_everyone(x, axis), dim)


def split_up(x, dim, size):
    dims = x.shape
    tiles = x.reshape(*dims[:dim], size, dims[dim] // size, *dims[dim + 1 :])
    return jnp.moveaxis(tiles, dim, 0)


def summed_on_arrival(x, axis, dim):
    tiles = split_up(x, dim, lax.axis_size(axis))
    arrived = lax.all_to_all(tiles, axis, split_axis=0, concat_axis=0, tiled=True)
    return arrived.sum(axis=0)


def summed_on_arrival_2(x, axis, dim):
    size = lax.axis_size(axis)
    tiles = lax.all_to_all(split_up(x, dim, size), axis, 0, 0, tiled=True)
    return jnp.sum(tiles.astype(jnp.float32), axis=0)


def side_by_side(arrays, axis, dim, along):
    columns = [a.reshape(*a.shape[:along], -1) for a in arrays]
    both = jnp.concatenate(columns, axis=along)
    filled, at, outs = (summed_on_arrival_2(both, axis, dim), 0, [])
    for a, column in zip(arrays, columns):
        section = filled[..., at : at + column.shape[along]]
        outs.append(section.reshape(*section.shape[:along], *a.shape[along:]))
        at += column.shape[along]
    return tuple(outs)


def rope_tables(positions, head_size):
    half_size = head_size // 2
    freqs = rope_base ** (-jnp.arange(half_size, dtype=jnp.float32) / half_size)
    angles = positions.astype(jnp.float32)[:, None] * freqs[None, :]
    return (jnp.cos(angles), jnp.sin(angles))


def rotate(values_in, cosine, sine):
    half_size = values_in.shape[-1] // 2
    first, second = (values_in[..., :half_size], values_in[..., half_size:])
    return jnp.concatenate(
        [first * cosine - second * sine, second * cosine + first * sine], axis=-1
    )


def unrotate(grad_out, cosine, sine):
    half_size = grad_out.shape[-1] // 2
    first, second = (grad_out[..., :half_size], grad_out[..., half_size:])
    return jnp.concatenate(
        [first * cosine + second * sine, second * cosine - first * sine], axis=-1
    )


def forward_fold(query_rows, row_pos):

    def forward_advance(carry, piece, start):
        row_top, row_total, weighted = carry
        key_part, value_part = piece
        scores = jnp.einsum("qd,kd->qk", query_rows, key_part, preferred_element_type=jnp.float32)
        key_pos = start + jnp.arange(key_part.shape[0], dtype=jnp.int32)
        allowed = key_pos[None, :] <= row_pos[:, None]
        scores = jnp.where(allowed, scores, -1e30)
        new_top = jnp.maximum(row_top, jnp.max(scores, axis=1))
        numbers = jnp.where(allowed, jnp.exp(scores - new_top[:, None]), 0.0)
        row_total = jnp.sum(numbers, axis=1)
        weighted = jnp.dot(
            numbers,
            value_part.astype(jnp.float32),
            precision=lax.Precision.HIGHEST,
            preferred_element_type=jnp.float32,
        )
        return (new_top, row_total, weighted)

    return forward_advance


def query_grad_fold(query_rows, row_pos, grad_flat, log_total, row_delta):

    def query_advance(grad_query, piece, start):
        key_part, value_part = piece
        scores = jnp.einsum("qd,kd->qk", query_rows, key_part, preferred_element_type=jnp.float32)
        key_pos = start + jnp.arange(key_part.shape[0], dtype=jnp.int32)
        allowed = key_pos[None, :] <= row_pos[:, None]
        probs = jnp.where(
            allowed, jnp.exp(jnp.where(allowed, scores, -1e30) - log_total[:, None]), 0.0
        )
        grad_probs = jnp.einsum(
            "qd,kd->qk", grad_flat, value_part, preferred_element_type=jnp.float32
        )
        grad_scores = (probs * (grad_probs - row_delta[:, None])).astype(jnp.bfloat16)
        return jnp.dot(grad_scores, key_part, preferred_element_type=jnp.float32)

    return query_advance


def key_grad_fold(key_rows, value_rows, key_pos, log_all, delta_all, heads_count):

    def key_advance(carry, piece, start):
        query_part, attn_grad_part = piece
        count = query_part.shape[0]
        scores = jnp.einsum("qd,kd->qk", query_part, key_rows, preferred_element_type=jnp.float32)
        query_pos = jnp.arange(count, dtype=jnp.int32) // heads_count
        allowed = key_pos[None, :] <= query_pos[:, None]
        probs = jnp.where(
            allowed, jnp.exp(jnp.where(allowed, scores, -1e30) - log_all[:, None]), 0.0
        )
        grad_values = jnp.einsum(
            "qk,qd->kd",
            probs.astype(jnp.bfloat16),
            attn_grad_part,
            preferred_element_type=jnp.float32,
        )
        grad_probs = jnp.einsum(
            "qd,kd->qk", attn_grad_part, value_rows, preferred_element_type=jnp.float32
        )
        grad_scores = (probs * (grad_probs - delta_all[:, None])).astype(jnp.bfloat16)
        grad_keys = jnp.einsum(
            "qk,qd->kd", grad_scores, query_part, preferred_element_type=jnp.float32
        )
        return (grad_keys, grad_values)

    return key_advance


def local(hidden_in, norm_gain, qkv_weight, attn_cotangent):
    rows_in = hidden_in[0]
    grad_attn = attn_cotangent[0]
    tokens_here = rows_in.shape[0]
    width = rows_in.shape[1]
    head_size = HD
    heads_count = HEADS
    qcols = heads_count * head_size
    scale = head_size ** (-0.5)
    weight_group, gain_group = sent_together((qkv_weight, norm_gain), "intra", 0, 1)
    weight_full, gain_full = sent_together((weight_group, gain_group), "inter", 0, 1)
    query_pos = lax.axis_index("intra") * tokens_here + jnp.arange(tokens_here, dtype=jnp.int32)
    row_pos = jnp.broadcast_to(query_pos[:, None], (tokens_here, heads_count)).reshape(
        tokens_here * heads_count
    )
    cosine, sine = rope_tables(query_pos, head_size)
    wide_rows = rows_in.astype(jnp.float32)
    inv_rms = lax.rsqrt(jnp.mean(wide_rows * wide_rows, axis=1, keepdims=True) + eps_norm)
    normed = (wide_rows * inv_rms * gain_full.astype(jnp.float32)[None, :]).astype(jnp.bfloat16)
    mixed = jnp.dot(normed, weight_full, preferred_element_type=jnp.float32)
    query_rows = (
        (
            rotate(
                mixed[:, :qcols].reshape(tokens_here, heads_count, head_size),
                cosine[:, None, :],
                sine[:, None, :],
            )
            * scale
        )
        .astype(jnp.bfloat16)
        .reshape(tokens_here * heads_count, head_size)
    )
    key_rows = rotate(mixed[:, qcols : qcols + head_size], cosine, sine).astype(jnp.bfloat16)
    value_rows = mixed[:, qcols + head_size :].astype(jnp.bfloat16)
    grad_flat = grad_attn.reshape(tokens_here * heads_count, head_size)
    flat_rows = tokens_here * heads_count
    forward_step = forward_fold(query_rows, row_pos)
    start_carry = (
        jnp.full((flat_rows,), -1e30, jnp.float32),
        jnp.zeros((flat_rows,), jnp.float32),
        jnp.zeros((flat_rows, head_size), jnp.float32),
    )
    key_all, value_all = in_one_piece((key_rows, value_rows), "intra", 0, 1)
    row_top, row_total, weighted = forward_step(start_carry, (key_all, value_all), 0)
    attn_flat = (weighted / row_total[:, None]).astype(jnp.bfloat16)
    log_total = row_top + jnp.log(row_total)
    row_delta = jnp.sum(grad_flat.astype(jnp.float32) * attn_flat.astype(jnp.float32), axis=1)
    query_step = query_grad_fold(query_rows, row_pos, grad_flat, log_total, row_delta)
    grad_query = query_step(jnp.zeros((flat_rows, head_size), jnp.float32), (key_all, value_all), 0)
    log_all, delta_all = gather_turned((log_total, row_delta), "intra", (0, 0))
    key_step = key_grad_fold(key_rows, value_rows, query_pos, log_all, delta_all, heads_count)
    grad_keys, grad_values = key_step(
        (
            jnp.zeros((tokens_here, head_size), jnp.float32),
            jnp.zeros((tokens_here, head_size), jnp.float32),
        ),
        in_one_piece((query_rows, grad_flat), "intra", 0, 1),
        jnp.int32(0),
    )
    query_back = (
        unrotate(
            grad_query.reshape(tokens_here, heads_count, head_size),
            cosine[:, None, :],
            sine[:, None, :],
        )
        * scale
    ).reshape(tokens_here, qcols)
    grad_mixed = jnp.concatenate(
        [query_back, unrotate(grad_keys, cosine, sine), grad_values], axis=1
    ).astype(jnp.bfloat16)
    weight_back, gain_back = (weight_full, gain_full)
    gain_wide = gain_back.astype(jnp.float32)[None, :]
    grad_normed = jnp.einsum(
        "tc,dc->td", grad_mixed, weight_back, preferred_element_type=jnp.float32
    )
    inner = jnp.sum(grad_normed * gain_wide * wide_rows, axis=1, keepdims=True)
    grad_rows = (
        gain_wide * grad_normed * inv_rms - wide_rows * inv_rms**3 / width * inner
    ).astype(jnp.bfloat16)
    gain_term = jnp.sum(grad_normed * wide_rows * inv_rms, axis=0)
    normed_cols = lax.all_to_all(normed, "intra", split_axis=1, concat_axis=0, tiled=True)
    group_term = lax.dot_general(
        normed_cols,
        gather_directly(grad_mixed, "intra", 0),
        (((0,), (0,)), ((), ())),
        preferred_element_type=jnp.float32,
    )
    term_low = lax.optimization_barrier(group_term.astype(jnp.bfloat16))
    gain_sums = summed_on_arrival(gain_term, "intra", 0)
    weight_grad, gain_grad = side_by_side(
        (term_low.astype(jnp.float32).astype(jnp.bfloat16), gain_sums.astype(jnp.bfloat16)),
        "inter",
        0,
        1,
    )
    return (attn_flat.reshape(tokens_here, qcols)[None], grad_rows[None], weight_grad, gain_grad)


def solution(mesh):
    return jax.shard_map(
        local,
        mesh=mesh,
        in_specs=(
            P("inter", "intra", None),
            P(("inter", "intra")),
            P(("inter", "intra"), None),
            P("inter", "intra", None),
        ),
        out_specs=(
            P("inter", "intra", None),
            P("inter", "intra", None),
            P(("intra", "inter"), None),
            P(("intra", "inter")),
        ),
        check_vma=False,
    )
```

profile of v0, /device:TPU:16, one launch (start us, length us, event | category | flops | bytes accessed | tf_op | source)
XLA Modules:
  0.0 335.2 jit_solution(8068869801132005356)
XLA Ops:
  8.8 30.7 %all_gather.15 = bf16[64,769]{1,0:T(8,128)(2,1)} all-gather(bf16[8,769]{1,0:T(8,128)(2,1)S(1)} %pad_maximum_fusion.4), channel_id=1, replica_groups=mesh['inter'=64,'intra'=8] {'intra'}, dimensions={0}, use_global_device_ids=true | all-gather | bytes 110736 | tf_op jit(solution)/shard_map/all_gather | solution.py:18
  42.6 2.6 copy.44
  46.1 96.7 %all-gather.3.cloned.1.call-done = bf16[4096,769]{1,0:T(8,128)(2,1)} async-done(((bf16[64,769]{1,0:T(8,128)(2,1)}), bf16[4096,769]{1,0:T(8,128)(2,1)}) %all-gather.3.cloned.1.call-update) | async-done | bytes 6299664 | tf_op jit(solution)/shard_map/all_gather | solution.py:18
  142.8 1.6 convert_reduce_fusion
  144.4 3.8 %fusion.2 = f32[128,768]{1,0:T(8,128)S(1)} fusion(bf16[4096,769]{1,0:T(8,128)(2,1)} %all-gather.3.cloned.1.call-done, bf16[1,128,4096]{2,1,0:T(8,128)(2,1)S(1)} %copy-done, f32[4096]{0:T(1024)S(1)} %convert_reduce_fusion, f32[128]{0:T(128)S(1)} %get-tuple-element.19), kind=kOutput, calls=%fused_computation.2 | convolution fusion | flops 807403520 | bytes 7750144 | tf_op jit(solution)/shard_map/dot_general | solution.py:202
  151.3 32.7 %all_gather.17 = bf16[1024,256]{1,0:T(8,128)(2,1)S(1)} all-gather(bf16[128,256]{1,0:T(8,128)(2,1)S(1)} %pad_maximum_fusion.3), channel_id=1, replica_groups=mesh['inter'=64,'intra'=8] {'intra'}, dimensions={0}, use_global_device_ids=true | all-gather | bytes 589824 | tf_op jit(solution)/shard_map/all_gather | solution.py:31
  185.2 1.3 fusion.20
  186.6 2.4 multiply_reduce_fusion
  189.0 2.6 fusion.23
  191.6 1.4 multiply_add_fusion
  193.4 1.5 multiply_convert_fusion
  194.9 4.3 %all-to-all-start = ((bf16[128,8,512]{0,2,1:T(8,128)(2,1)}), bf16[128,8,512]{0,2,1:T(8,128)(2,1)}, u32[]{:S(2)}, u32[]{:S(2)}) async-start(bf16[128,8,512]{0,2,1:T(8,128)(2,1)} %multiply_convert_fusion), calls=%async_computation | async-start | bytes 2097152 | tf_op jit(solution)/shard_map/all_to_all | solution.py:263
  199.2 43.5 %all_gather.19 = f32[4096,2]{0,1:T(2,128)S(1)} all-gather(f32[512,2]{0,1:T(2,128)S(1)} %pad_maximum_fusion.5), channel_id=1, replica_groups=mesh['inter'=64,'intra'=8] {'intra'}, dimensions={0}, use_global_device_ids=true | all-gather | bytes 36864 | tf_op jit(solution)/shard_map/all_gather | solution.py:37
  242.7 3.3 fusion.6
  246.7 3.0 fusion.22
  250.2 6.3 %fusion.18 = (f32[4096]{0:T(1024)S(1)}, f32[128]{0:T(128)S(1)}, f32[128,4096]{1,0:T(8,128)}) fusion(bf16[1,128,4096]{2,1,0:T(8,128)(2,1)S(1)} %copy-done, f32[128]{0:T(128)S(1)} %copy-done.21, f32[4096]{0:T(1024)S(1)} %convert_reduce_fusion, bf16[128,768]{1,0:T(8,128)(2,1)S(1)} %pad_maximum_fusion.2, bf16[4096,769]{1,0:T(8,128)(2,1)} %all-gather.3.cloned.1.call-done), kind=kOutput, calls=%fused_computation.26 | convolution fusion | flops 808972160 | bytes 9667584 | tf_op jit(solution)/shard_map/tc,dc->td/dot_general | solution.py:255
  256.6 8.6 %all_to_all.32 = f32[8,1,512]{2,1,0:T(1,128)S(1)} all-to-all(f32[8,1,512]{2,1,0:T(1,128)S(1)} %bitcast.67), channel_id=1, replica_groups=mesh['inter'=64,'intra'=8] {'intra'}, dimensions={0} | all-to-all | bytes 32768 | tf_op jit(solution)/shard_map/all_to_all | solution.py:68
  265.1 1.3 broadcast_in_dim.59
  266.4 3.6 %all-to-all-start.1 = ((bf16[8,128,768]{2,1,0:T(8,128)(2,1)}), bf16[8,128,768]{2,1,0:T(8,128)(2,1)S(1)}, u32[]{:S(2)}, u32[]{:S(2)}) async-start(bf16[8,128,768]{2,1,0:T(8,128)(2,1)} %broadcast_in_dim.59), calls=%async_computation.1 | async-start | bytes 3145728 | tf_op jit(solution)/shard_map/all_to_all | solution.py:53
  270.3 14.0 %all-to-all-done.1 = bf16[8,128,768]{2,1,0:T(8,128)(2,1)S(1)} async-done(((bf16[8,128,768]{2,1,0:T(8,128)(2,1)}), bf16[8,128,768]{2,1,0:T(8,128)(2,1)S(1)}, u32[]{:S(2)}, u32[]{:S(2)}) %all-to-all-start.1) | async-done | bytes 1572896 | tf_op jit(solution)/shard_map/all_to_all | solution.py:53
  284.3 2.2 bitcast_convert_fusion
  287.5 11.4 %all-to-all-start.3 = ((bf16[64,8,769]{2,1,0:T(8,128)(2,1)}), bf16[64,8,769]{2,1,0:T(8,128)(2,1)S(1)}, u32[]{:S(2)}, u32[]{:S(2)}) async-start(bf16[64,8,769]{2,1,0:T(8,128)(2,1)} %pad_maximum_fusion), calls=%async_computation.3 | async-start | bytes 1835008 | tf_op jit(solution)/shard_map/all_to_all | solution.py:74
  299.8 3.2 fusion.26
  302.9 24.0 %all-to-all-done.3 = bf16[64,8,769]{2,1,0:T(8,128)(2,1)S(1)} async-done(((bf16[64,8,769]{2,1,0:T(8,128)(2,1)}), bf16[64,8,769]{2,1,0:T(8,128)(2,1)S(1)}, u32[]{:S(2)}, u32[]{:S(2)}) %all-to-all-start.3) | async-done | bytes 787488 | tf_op jit(solution)/shard_map/all_to_all | solution.py:74
  (97 shorter events, 14.9 us)
Async XLA Ops:
  7.2 38.1 %copy-start = (bf16[1,128,4096]{2,1,0:T(8,128)(2,1)S(1)}, bf16[1,128,4096]{2,1,0:T(8,128)(2,1)}, u32[]{:S(2)}) copy-start(bf16[1,128,4096]{2,1,0:T(8,128)(2,1)} %param.4) | copy-start | bytes 3145732
  7.2 135.6 %all-gather.3.cloned.1.call-start = ((), (), s32[]{:S(2)}) async-start(), calls=%async_computation.4 | async-start | bytes 7454720 | tf_op jit(solution)/shard_map/all_gather | solution.py:18
  39.5 203.2 %all-gather.5.cloned.1.call-start = ((), (), s32[]{:S(2)}) async-start(), calls=%async_computation.5 | async-start | bytes 2359296 | tf_op jit(solution)/shard_map/all_gather | solution.py:31
  45.3 103.1 %copy-start.15 = (f32[128]{0:T(128)}, f32[128]{0:T(128)S(1)}, u32[]{:S(2)}) copy-start(f32[128]{0:T(128)S(1)} %fusion.77) | copy-start | bytes 1540
  45.3 103.1 %copy-start.17 = (f32[64]{0:T(128)}, f32[64]{0:T(128)S(1)}, u32[]{:S(2)}) copy-start(f32[64]{0:T(128)S(1)} %multiply_power_fusion) | copy-start | bytes 772
  46.1 102.1 %copy-start.19 = (f32[128]{0:T(128)}, f32[128]{0:T(128)S(1)}, u32[]{:S(2)}) copy-start(f32[128]{0:T(128)S(1)} %get-tuple-element.19) | copy-start | bytes 1540
  148.2 3.0 copy-start.4
  183.9 2.6 copy-start.3
  183.9 2.6 copy-start.10
  183.9 2.7 copy-start.12
  189.0 4.2 %copy-start.11 = (f32[8,512]{1,0:T(8,128)S(1)}, f32[8,512]{1,0:T(8,128)}, u32[]{:S(2)}) copy-start(f32[8,512]{1,0:T(8,128)} %reshape.205) | copy-start | bytes 49156
  193.4 49.3 %copy-start.6 = (bf16[128,64]{1,0:T(8,128)(2,1)S(1)}, bf16[128,64]{1,0:T(8,128)(2,1)}, u32[]{:S(2)}) copy-start(bf16[128,64]{1,0:T(8,128)(2,1)} %copy-done.5) | copy-start | bytes 49156
  193.4 49.3 %copy-start.8 = (bf16[128,64]{1,0:T(8,128)(2,1)S(1)}, bf16[128,64]{1,0:T(8,128)(2,1)}, u32[]{:S(2)}) copy-start(bf16[128,64]{1,0:T(8,128)(2,1)} %copy-done.7) | copy-start | bytes 49156
  193.4 49.3 %copy-start.14 = (s32[4096]{0:T(1024)S(1)}, s32[4096]{0:T(1024)}, u32[]{:S(2)}) copy-start(s32[4096]{0:T(1024)} %add_select_fusion) | copy-start | bytes 49156
  193.4 49.3 %copy-start.24 = (s32[128]{0:T(128)S(1)}, s32[128]{0:T(128)}, u32[]{:S(2)}) copy-start(s32[128]{0:T(128)} %copy-done.23) | copy-start | bytes 1540
  194.9 61.7 %all-to-all-start = ((bf16[128,8,512]{0,2,1:T(8,128)(2,1)}), bf16[128,8,512]{0,2,1:T(8,128)(2,1)}, u32[]{:S(2)}, u32[]{:S(2)}) async-start(bf16[128,8,512]{0,2,1:T(8,128)(2,1)} %multiply_convert_fusion), calls=%async_computation | async-start | bytes 2097152 | tf_op jit(solution)/shard_map/all_to_all | solution.py:263
  242.7 3.3 copy-start.2
  246.7 3.1 copy-start.16
  246.7 3.1 copy-start.18
  246.7 3.5 %copy-start.21 = (f32[128]{0:T(128)S(1)}, f32[128]{0:T(128)}, u32[]{:S(2)}) copy-start(f32[128]{0:T(128)} %copy-done.19) | copy-start | bytes 1540
  266.4 17.9 %all-to-all-start.1 = ((bf16[8,128,768]{2,1,0:T(8,128)(2,1)}), bf16[8,128,768]{2,1,0:T(8,128)(2,1)S(1)}, u32[]{:S(2)}, u32[]{:S(2)}) async-start(bf16[8,128,768]{2,1,0:T(8,128)(2,1)} %broadcast_in_dim.59), calls=%async_computation.1 | async-start | bytes 3145728 | tf_op jit(solution)/shard_map/all_to_all | solution.py:53
  286.5 12.4 %copy-start.9 = (bf16[512,128]{0,1:T(8,128)(2,1)S(1)}, bf16[512,128]{0,1:T(8,128)(2,1)}, u32[]{:S(2)}) copy-start(bf16[512,128]{0,1:T(8,128)(2,1)} %get-tuple-element.23) | copy-start | bytes 393220
  286.5 13.3 %copy-start.22 = (f32[128]{0:T(128)S(1)}, f32[128]{0:T(128)}, u32[]{:S(2)}) copy-start(f32[128]{0:T(128)} %get-tuple-element.18) | copy-start | bytes 1540
  287.5 39.5 %all-to-all-start.3 = ((bf16[64,8,769]{2,1,0:T(8,128)(2,1)}), bf16[64,8,769]{2,1,0:T(8,128)(2,1)S(1)}, u32[]{:S(2)}, u32[]{:S(2)}) async-start(bf16[64,8,769]{2,1,0:T(8,128)(2,1)} %pad_maximum_fusion), calls=%async_computation.3 | async-start | bytes 1835008 | tf_op jit(solution)/shard_map/all_to_all | solution.py:74
  (6 other events, 11.6 us)
Sparse Core Ops, SparseCore 0:
  39.6 103.1 all-gather.2
  150.0 67.2 all-gather.4
where the time goes:
time: 336 us; the launch traced here: 335 us
  waiting for transfers between devices  135 us (40%)
  blocking collectives  115 us (34%)
  matrix products  25.5 us (8%)
  starting transfers between devices  19.3 us (6%)
  other arithmetic  14.6 us (4%)
  between operations  14.5 us (4%)
  local copies, waits for them, and re-layouts  11.2 us (3%)
    all_gather x1, waiting for transfers between devices, sent_together(): filled = lax.all_gather(both, axis, axis=dim, tiled=True)  96.7 us
    all_gather x1, blocking collectives, gather_turned(): filled, at, outs = (lax.all_gather(both, axis, axis=0, tiled=True), 0, [])  43.5 us
    all_gather x1, blocking collectives, in_one_piece(): lax.all_gather(both, axis, axis=dim, tiled=True)  32.7 us
    all_gather x1, blocking collectives, sent_together(): filled = lax.all_gather(both, axis, axis=dim, tiled=True)  30.7 us
    all_to_all x1, waiting for transfers between devices, summed_on_arrival_2(): tiles = lax.all_to_all(split_up(x, dim, size), axis, 0, 0, tiled=True)  24 us
    all_to_all x1, waiting for transfers between devices, from_everyone(): return lax.all_to_all(copies, axis, split_axis=0, concat_axis=0, tiled=True)  14 us
    all_to_all x1, starting transfers between devices, summed_on_arrival_2(): tiles = lax.all_to_all(split_up(x, dim, size), axis, 0, 0, tiled=True)  11.4 us
    all_to_all x1, blocking collectives, summed_on_arrival(): lax.all_to_all(tiles, axis, split_axis=0, concat_axis=0, tiled=True)  8.56 us
  transfers between devices with their start and end apart: 5, of which 3 were waited for; matrix products, arithmetic and copies ran while one was open for 11% of the time, Pallas kernels for 0%

commit v1 on v0

--- a/solution.py
+++ b/solution.py
@@ -34,7 +34,13 @@
 def gather_turned(arrays, axis, dims):
     turned = [jnp.moveaxis(a, dim, 0) for a, dim in zip(arrays, dims)]
     both = jnp.concatenate([t.reshape(len(t), -1) for t in turned], axis=1)
-    filled, at, outs = (lax.all_gather(both, axis, axis=0, tiled=True), 0, [])
+    filled, at, outs = (
+        jnp.concatenate(
+            lax.all_to_all(jnp.stack([both] * lax.axis_size(axis)), axis, 0, 0), axis=0
+        ),
+        0,
+        [],
+    )
     for t, dim in zip(turned, dims):
         section = filled[:, at : at + t[0].size].reshape(-1, *t.shape[1:])
         outs.append(jnp.moveaxis(section, 0, dim))

time: 336 us -> 315 us (0.938)
  blocking collectives: 115 us -> 73.5 us
  waiting for transfers between devices: 135 us -> 145 us
  starting transfers between devices: 19.3 us -> 28 us
    all_gather x1 -> x0, blocking collectives: 43.5 us -> none  [gather_turned(): filled, at, outs = (lax.all_gather(both, axis, axis=0, tiled=True), 0, [])]
    all_to_all x1, waiting for transfers between devices: 14 us -> 19.1 us  [from_everyone(): return lax.all_to_all(copies, axis, split_axis=0, concat_axis=0, tiled=True)]
    all_gather x1, waiting for transfers between devices: 0.02 us -> 4.89 us  [in_one_piece(): lax.all_gather(both, axis, axis=dim, tiled=True)]
    all_to_all x0 -> x1, starting transfers between devices: none -> 3.95 us  [gather_turned(): lax.all_to_all(jnp.stack([both] * lax.axis_size(axis)), axis, 0, 0)]
    all_to_all x1, starting transfers between devices: 11.4 us -> 14.8 us  [summed_on_arrival_2(): tiles = lax.all_to_all(split_up(x, dim, size), axis, 0, 0, tiled=True)]
  transfers between devices with their start and end apart: 5 -> 6, of which waited for: 3 -> 4; matrix products, arithmetic and copies ran while one was open for 11% -> 12% of each run, Pallas kernels for 0% -> 0%
where the time goes in v1:
time: 315 us; the launch traced here: 314 us
  waiting for transfers between devices  145 us (46%)
  blocking collectives  73.5 us (23%)
  starting transfers between devices  28 us (9%)
  matrix products  25.5 us (8%)
  other arithmetic  15.6 us (5%)
  between operations  14.5 us (5%)
  local copies, waits for them, and re-layouts  12.5 us (4%)
    all_gather x1, waiting for transfers between devices, sent_together(): filled = lax.all_gather(both, axis, axis=dim, tiled=True)  96.7 us
    all_gather x1, blocking collectives, in_one_piece(): lax.all_gather(both, axis, axis=dim, tiled=True)  32.6 us
    all_gather x1, blocking collectives, sent_together(): filled = lax.all_gather(both, axis, axis=dim, tiled=True)  30.7 us
    all_to_all x1, waiting for transfers between devices, summed_on_arrival_2(): tiles = lax.all_to_all(split_up(x, dim, size), axis, 0, 0, tiled=True)  24 us
    all_to_all x1, waiting for transfers between devices, from_everyone(): return lax.all_to_all(copies, axis, split_axis=0, concat_axis=0, tiled=True)  19.1 us
    all_to_all x1, starting transfers between devices, summed_on_arrival_2(): tiles = lax.all_to_all(split_up(x, dim, size), axis, 0, 0, tiled=True)  14.8 us
    all_to_all x1, blocking collectives, summed_on_arrival(): lax.all_to_all(tiles, axis, split_axis=0, concat_axis=0, tiled=True)  10.1 us
    dot_general x1, matrix products, local(): jnp.einsum('tc,dc->td', grad_mixed, weight_back, preferred_element_type=j...  6.4 us
  transfers between devices with their start and end apart: 6, of which 4 were waited for; matrix products, arithmetic and copies ran while one was open for 12% of the time, Pallas kernels for 0%

profile of v1, /device:TPU:16, one launch (start us, length us, event | category | flops | bytes accessed | tf_op | source)
XLA Modules:
  0.0 314.4 jit_solution(15494267730667985198)
XLA Ops:
  8.8 30.7 %all_gather.12 = bf16[64,769]{1,0:T(8,128)(2,1)} all-gather(bf16[8,769]{1,0:T(8,128)(2,1)S(1)} %pad_maximum_fusion.4), channel_id=1, replica_groups=mesh['inter'=64,'intra'=8] {'intra'}, dimensions={0}, use_global_device_ids=true | all-gather | bytes 110736 | tf_op jit(solution)/shard_map/all_gather | solution.py:18
  42.6 2.6 copy.53
  46.1 96.7 %all-gather.3.cloned.1.call-done = bf16[4096,769]{1,0:T(8,128)(2,1)} async-done(((bf16[64,769]{1,0:T(8,128)(2,1)}), bf16[4096,769]{1,0:T(8,128)(2,1)}) %all-gather.3.cloned.1.call-update) | async-done | bytes 6299664 | tf_op jit(solution)/shard_map/all_gather | solution.py:18
  142.8 1.6 convert_reduce_fusion
  144.4 3.8 %fusion.2 = f32[128,768]{1,0:T(8,128)S(1)} fusion(bf16[4096,769]{1,0:T(8,128)(2,1)} %all-gather.3.cloned.1.call-done, bf16[1,128,4096]{2,1,0:T(8,128)(2,1)S(1)} %copy-done, f32[4096]{0:T(1024)S(1)} %convert_reduce_fusion, f32[128]{0:T(128)S(1)} %get-tuple-element.19), kind=kOutput, calls=%fused_computation.2 | convolution fusion | flops 807403520 | bytes 7750144 | tf_op jit(solution)/shard_map/dot_general | solution.py:208
  151.2 32.6 %all_gather.14 = bf16[1024,256]{1,0:T(8,128)(2,1)S(1)} all-gather(bf16[128,256]{1,0:T(8,128)(2,1)S(1)} %pad_maximum_fusion.3), channel_id=1, replica_groups=mesh['inter'=64,'intra'=8] {'intra'}, dimensions={0}, use_global_device_ids=true | all-gather | bytes 589824 | tf_op jit(solution)/shard_map/all_gather | solution.py:31
  186.4 2.4 multiply_reduce_fusion
  189.5 4.0 %all-to-all-start = ((f32[8,512,2]{1,2,0:T(2,128)}), f32[8,512,2]{1,2,0:T(2,128)}, u32[]{:S(2)}, u32[]{:S(2)}) async-start(f32[8,512,2]{1,2,0:T(2,128)} %stack.2), calls=%async_computation | async-start | bytes 65536 | tf_op jit(solution)/shard_map/all_to_all | solution.py:39
  193.5 2.6 fusion.23
  196.0 1.3 multiply_add_fusion
  197.4 2.7 multiply_convert_fusion
  200.3 5.6 %all-to-all-start.1 = ((bf16[128,8,512]{0,2,1:T(8,128)(2,1)}), bf16[128,8,512]{0,2,1:T(8,128)(2,1)}, u32[]{:S(2)}, u32[]{:S(2)}) async-start(bf16[128,8,512]{0,2,1:T(8,128)(2,1)} %multiply_convert_fusion), calls=%async_computation.1 | async-start | bytes 2097152 | tf_op jit(solution)/shard_map/all_to_all | solution.py:269
  206.8 4.9 %all-gather.5.cloned.1.call-done = bf16[4096,256]{1,0:T(8,128)(2,1)} async-done(((bf16[512,256]{1,0:T(8,128)(2,1)}), bf16[4096,256]{1,0:T(8,128)(2,1)}) %all-gather.5.cloned.1.call-update) | async-done | bytes 2097168 | tf_op jit(solution)/shard_map/all_gather | solution.py:31
  211.7 3.3 %fusion.6 = f32[4096,128]{1,0:T(8,128)S(1)} fusion(f32[4096]{0:T(1024)S(1)} %bitcast.69, s32[128]{0:T(128)S(1)} %copy-done.23, s32[4096]{0:T(1024)S(1)} %copy-done.13, bf16[4096,256]{1,0:T(8,128)(2,1)} %all-gather.5.cloned.1.call-done, bf16[128,64]{1,0:T(8,128)(2,1)S(1)} %copy-done.7, bf16[128,64]{1,0:T(8,128)(2,1)S(1)} %copy-done.5), kind=kOutput, calls=%fused_computation.7 | convolution fusion | flops 136380416 | bytes 3211776 | tf_op jit(solution)/shard_map/qd,kd->qk/dot_general | solution.py:165
  215.7 3.0 fusion.22
  219.2 6.4 %fusion.18 = (f32[4096]{0:T(1024)S(1)}, f32[128]{0:T(128)S(1)}, f32[128,4096]{1,0:T(8,128)}) fusion(bf16[1,128,4096]{2,1,0:T(8,128)(2,1)S(1)} %copy-done, f32[128]{0:T(128)S(1)} %copy-done.20, f32[4096]{0:T(1024)S(1)} %convert_reduce_fusion, bf16[128,768]{1,0:T(8,128)(2,1)S(1)} %pad_maximum_fusion.2, bf16[4096,769]{1,0:T(8,128)(2,1)} %all-gather.3.cloned.1.call-done), kind=kOutput, calls=%fused_computation.26 | convolution fusion | flops 808972160 | bytes 9667584 | tf_op jit(solution)/shard_map/tc,dc->td/dot_general | solution.py:261
  225.6 10.1 %all_to_all.37 = f32[8,1,512]{2,1,0:T(1,128)S(1)} all-to-all(f32[8,1,512]{2,1,0:T(1,128)S(1)} %bitcast.68), channel_id=1, replica_groups=mesh['inter'=64,'intra'=8] {'intra'}, dimensions={0} | all-to-all | bytes 32768 | tf_op jit(solution)/shard_map/all_to_all | solution.py:74
  235.8 1.3 broadcast_in_dim.59
  237.0 3.6 %all-to-all-start.2 = ((bf16[8,128,768]{2,1,0:T(8,128)(2,1)}), bf16[8,128,768]{2,1,0:T(8,128)(2,1)S(1)}, u32[]{:S(2)}, u32[]{:S(2)}) async-start(bf16[8,128,768]{2,1,0:T(8,128)(2,1)} %broadcast_in_dim.59), calls=%async_computation.2 | async-start | bytes 3145728 | tf_op jit(solution)/shard_map/all_to_all | solution.py:59
  240.9 19.1 %all-to-all-done.2 = bf16[8,128,768]{2,1,0:T(8,128)(2,1)S(1)} async-done(((bf16[8,128,768]{2,1,0:T(8,128)(2,1)}), bf16[8,128,768]{2,1,0:T(8,128)(2,1)S(1)}, u32[]{:S(2)}, u32[]{:S(2)}) %all-to-all-start.2) | async-done | bytes 1572896 | tf_op jit(solution)/shard_map/all_to_all | solution.py:59
  260.0 2.2 bitcast_convert_fusion
  263.2 14.8 %all-to-all-start.4 = ((bf16[64,8,769]{2,1,0:T(8,128)(2,1)}), bf16[64,8,769]{2,1,0:T(8,128)(2,1)S(1)}, u32[]{:S(2)}, u32[]{:S(2)}) async-start(bf16[64,8,769]{2,1,0:T(8,128)(2,1)} %pad_maximum_fusion), calls=%async_computation.4 | async-start | bytes 1835008 | tf_op jit(solution)/shard_map/all_to_all | solution.py:80
  278.9 3.2 %fusion.26 = bf16[1,128,4096]{2,1,0:T(8,128)(2,1)} fusion(bf16[1,128,4096]{2,1,0:T(8,128)(2,1)S(1)} %copy-done, f32[128,4096]{1,0:T(8,128)} %get-tuple-element.24, f32[128]{0:T(128)S(1)} %broadcast_multiply_fusion, f32[128]{0:T(128)S(1)} %copy-done.21, f32[4096]{0:T(1024)S(1)} %convert_reduce_fusion, f32[128]{0:T(128)S(1)} %copy-done.20), kind=kLoop, calls=%fused_computation.41 | loop fusion | flops 3670016 | bytes 4212224 | tf_op jit(solution)/shard_map/broadcast_in_dim | solution.py:284
  282.1 24.0 %all-to-all-done.4 = bf16[64,8,769]{2,1,0:T(8,128)(2,1)S(1)} async-done(((bf16[64,8,769]{2,1,0:T(8,128)(2,1)}), bf16[64,8,769]{2,1,0:T(8,128)(2,1)S(1)}, u32[]{:S(2)}, u32[]{:S(2)}) %all-to-all-start.4) | async-done | bytes 787488 | tf_op jit(solution)/shard_map/all_to_all | solution.py:80
  (97 shorter events, 17.4 us)
Async XLA Ops:
  7.2 38.1 %copy-start = (bf16[1,128,4096]{2,1,0:T(8,128)(2,1)S(1)}, bf16[1,128,4096]{2,1,0:T(8,128)(2,1)}, u32[]{:S(2)}) copy-start(bf16[1,128,4096]{2,1,0:T(8,128)(2,1)} %param.4) | copy-start | bytes 3145732
  7.2 135.6 %all-gather.3.cloned.1.call-start = ((), (), s32[]{:S(2)}) async-start(), calls=%async_computation.5 | async-start | bytes 7454720 | tf_op jit(solution)/shard_map/all_gather | solution.py:18
  39.5 172.2 %all-gather.5.cloned.1.call-start = ((), (), s32[]{:S(2)}) async-start(), calls=%async_computation.6 | async-start | bytes 2359296 | tf_op jit(solution)/shard_map/all_gather | solution.py:31
  45.2 103.1 %copy-start.14 = (f32[128]{0:T(128)}, f32[128]{0:T(128)S(1)}, u32[]{:S(2)}) copy-start(f32[128]{0:T(128)S(1)} %fusion.77) | copy-start | bytes 1540
  45.2 103.1 %copy-start.16 = (f32[64]{0:T(128)}, f32[64]{0:T(128)S(1)}, u32[]{:S(2)}) copy-start(f32[64]{0:T(128)S(1)} %multiply_power_fusion) | copy-start | bytes 772
  46.1 102.1 %copy-start.18 = (f32[128]{0:T(128)}, f32[128]{0:T(128)S(1)}, u32[]{:S(2)}) copy-start(f32[128]{0:T(128)S(1)} %get-tuple-element.19) | copy-start | bytes 1540
  148.2 3.0 copy-start.3
  186.4 7.0 %copy-start.12 = (s32[512]{0:T(512)S(1)}, s32[512]{0:T(512)}, u32[]{:S(2)}) copy-start(s32[512]{0:T(512)} %le.15) | copy-start | bytes 6148
  189.5 10.9 %all-to-all-start = ((f32[8,512,2]{1,2,0:T(2,128)}), f32[8,512,2]{1,2,0:T(2,128)}, u32[]{:S(2)}, u32[]{:S(2)}) async-start(f32[8,512,2]{1,2,0:T(2,128)} %stack.2), calls=%async_computation | async-start | bytes 65536 | tf_op jit(solution)/shard_map/all_to_all | solution.py:39
  193.4 3.9 %copy-start.10 = (f32[8,512]{1,0:T(8,128)S(1)}, f32[8,512]{1,0:T(8,128)}, u32[]{:S(2)}) copy-start(f32[8,512]{1,0:T(8,128)} %reshape.211) | copy-start | bytes 49156
  193.5 3.9 %copy-start.19 = (f32[128]{0:T(128)S(1)}, f32[128]{0:T(128)}, u32[]{:S(2)}) copy-start(f32[128]{0:T(128)} %copy-done.18) | copy-start | bytes 1540
  200.1 11.6 %copy-start.5 = (bf16[128,64]{1,0:T(8,128)(2,1)S(1)}, bf16[128,64]{1,0:T(8,128)(2,1)}, u32[]{:S(2)}) copy-start(bf16[128,64]{1,0:T(8,128)(2,1)} %copy-done.4) | copy-start | bytes 49156
  200.1 11.6 %copy-start.7 = (bf16[128,64]{1,0:T(8,128)(2,1)S(1)}, bf16[128,64]{1,0:T(8,128)(2,1)}, u32[]{:S(2)}) copy-start(bf16[128,64]{1,0:T(8,128)(2,1)} %copy-done.6) | copy-start | bytes 49156
  200.1 11.6 %copy-start.13 = (s32[4096]{0:T(1024)S(1)}, s32[4096]{0:T(1024)}, u32[]{:S(2)}) copy-start(s32[4096]{0:T(1024)} %add_select_fusion) | copy-start | bytes 49156
  200.1 11.6 %copy-start.23 = (s32[128]{0:T(128)S(1)}, s32[128]{0:T(128)}, u32[]{:S(2)}) copy-start(s32[128]{0:T(128)} %copy-done.22) | copy-start | bytes 1540
  200.3 25.3 %all-to-all-start.1 = ((bf16[128,8,512]{0,2,1:T(8,128)(2,1)}), bf16[128,8,512]{0,2,1:T(8,128)(2,1)}, u32[]{:S(2)}, u32[]{:S(2)}) async-start(bf16[128,8,512]{0,2,1:T(8,128)(2,1)} %multiply_convert_fusion), calls=%async_computation.1 | async-start | bytes 2097152 | tf_op jit(solution)/shard_map/all_to_all | solution.py:269
  211.7 3.3 %copy-start.1 = (bf16[4096,256]{1,0:T(8,128)(2,1)S(1)}, bf16[4096,256]{1,0:T(8,128)(2,1)}, u32[]{:S(2)}) copy-start(bf16[4096,256]{1,0:T(8,128)(2,1)} %all-gather.5.cloned.1.call-done) | copy-start | bytes 6291460
  215.7 3.1 copy-start.15
  215.7 3.1 copy-start.17
  215.7 3.5 %copy-start.20 = (f32[128]{0:T(128)S(1)}, f32[128]{0:T(128)}, u32[]{:S(2)}) copy-start(f32[128]{0:T(128)} %copy-done.18) | copy-start | bytes 1540
  237.0 23.0 %all-to-all-start.2 = ((bf16[8,128,768]{2,1,0:T(8,128)(2,1)}), bf16[8,128,768]{2,1,0:T(8,128)(2,1)S(1)}, u32[]{:S(2)}, u32[]{:S(2)}) async-start(bf16[8,128,768]{2,1,0:T(8,128)(2,1)} %broadcast_in_dim.59), calls=%async_computation.2 | async-start | bytes 3145728 | tf_op jit(solution)/shard_map/all_to_all | solution.py:59
  262.2 15.8 %copy-start.8 = (bf16[512,128]{0,1:T(8,128)(2,1)S(1)}, bf16[512,128]{0,1:T(8,128)(2,1)}, u32[]{:S(2)}) copy-start(bf16[512,128]{0,1:T(8,128)(2,1)} %get-tuple-element.23) | copy-start | bytes 393220
  262.2 16.6 %copy-start.21 = (f32[128]{0:T(128)S(1)}, f32[128]{0:T(128)}, u32[]{:S(2)}) copy-start(f32[128]{0:T(128)} %get-tuple-element.18) | copy-start | bytes 1540
  263.2 42.9 %all-to-all-start.4 = ((bf16[64,8,769]{2,1,0:T(8,128)(2,1)}), bf16[64,8,769]{2,1,0:T(8,128)(2,1)S(1)}, u32[]{:S(2)}, u32[]{:S(2)}) async-start(bf16[64,8,769]{2,1,0:T(8,128)(2,1)} %pad_maximum_fusion), calls=%async_computation.4 | async-start | bytes 1835008 | tf_op jit(solution)/shard_map/all_to_all | solution.py:80
  (6 other events, 13.3 us)
Sparse Core Ops, SparseCore 0:
  39.6 103.1 all-gather.2
  150.0 61.6 all-gather.4
